TPU v7x, 32 devices: a whole 2x2x4 slice. The times are simulated.
32 devices in a mesh: section: 4 (over y, core), tp: 8 (over z, x).
Axes of the slice: x: 2, y: 2, z: 4, core: 2. Of those that a mesh axis runs over, the one named last changes fastest.
Arguments:
- token_ids: int32 [2, 128], replicated, may hold values from 0 to 65535
- alpha_num: int32 [1], replicated, may hold values from 3 to 7
- embed_table: bfloat16 [65536, 8192], P('section', 'tp'), may hold values from -6 to 6
- norm_gain: float32 [4, 8192], P('section'), may hold values from 0.5 to 1.5
- w_query: bfloat16 [4, 8192, 4096], P('section', None, 'tp'), may hold values from -4 to 4
- w_key: bfloat16 [4, 8192, 512], P('section', None, 'tp'), may hold values from -4 to 4
- w_value: bfloat16 [4, 8192, 512], P('section', None, 'tp'), may hold values from -0.0625 to 0.0625
- w_out: bfloat16 [4, 4096, 8192], P('section', 'tp'), may hold values from -0.09375 to 0.09375
Outputs:
- layer_out: bfloat16 [4, 2, 128, 8192], P('section', None, 'tp')
- scales_in: float32 [4, 8192], P('section')
- scales_out: float32 [4, 4096], P('section', 'tp')
- smoothed_q: bfloat16 [4, 8192, 4096], P('section', None, 'tp')
- smoothed_k: bfloat16 [4, 8192, 512], P('section', None, 'tp')
- smoothed_v: bfloat16 [4, 8192, 512], P('section', None, 'tp')
All inputs are finite; a program needn't handle non-finite values.
Results may differ from a plain program's by a relative error of at most 0.028.
Values may be sent and summed in bfloat16 or wider, within the bound.
A program may use at most 128 MiB of HBM per device.

v0:
```python
import math

import jax
import jax.numpy as jnp
from jax import lax
from jax.sharding import PartitionSpec as P

KV_HEADS = 4
HEAD_DIM = 128


norm_eps = 1e-05
stat_eps = 1e-05
rope_base = 500000.0


def shifted(value, axis, steps):
    count = lax.axis_size(axis)
    first, last = (max(0, -steps), min(count, count - steps))
    return lax.ppermute(value, axis, [(source, source + steps) for source in range(first, last)])


def rope_tables(length, head_size):
    halves = head_size // 2
    freqs = jnp.exp(-math.log(rope_base) * 2.0 * jnp.arange(halves, dtype=jnp.float32) / head_size)
    angles = jnp.arange(length, dtype=jnp.float32)[:, None] * freqs[None, :]
    return (jnp.cos(angles), jnp.sin(angles))


def rotate(values, cosine, sine):
    halves = values.shape[-1] // 2
    lower = values[..., :halves]
    upper = values[..., halves:]
    cos_rows = cosine[:, None, :]
    sin_rows = sine[:, None, :]
    return jnp.concatenate(
        [lower * cos_rows - upper * sin_rows, upper * cos_rows + lower * sin_rows], axis=-1
    )


def smoothing(act_peak, weight_peak, alpha_exp):
    return jnp.exp(
        alpha_exp * jnp.log(act_peak + stat_eps)
        - (1.0 - alpha_exp) * jnp.log(weight_peak + stat_eps)
    )


def rms_normed(resid, gain_row):
    values = resid.astype(jnp.float32)
    square = jnp.mean(values * values, axis=1, keepdims=True)
    return (values * lax.rsqrt(square + norm_eps) * gain_row[None, :]).astype(jnp.bfloat16)


def shards(token_ids, alpha_num, embed_table, norm_gain, w_query, w_key, w_value, w_out):
    tp_count = lax.axis_size("tp")
    section_count = lax.axis_size("section")
    section_index = lax.axis_index("section")
    tp_index = lax.axis_index("tp")
    micros, length = token_ids.shape
    vocab_rows = embed_table.shape[0]
    own_rows = length // tp_count
    gain_row = norm_gain[0]
    query_cols = w_query.shape[2]
    kv_cols = w_key.shape[2]
    heads_here = query_cols // HEAD_DIM
    head_numbers = tp_index * heads_here + jnp.arange(heads_here, dtype=jnp.int32)
    selector = (
        head_numbers[:, None] % KV_HEADS == jnp.arange(KV_HEADS, dtype=jnp.int32)[None, :]
    ).astype(jnp.bfloat16)
    local_ids = token_ids - section_index * vocab_rows
    inside = (local_ids >= 0) & (local_ids < vocab_rows)
    picked = jnp.take(embed_table, jnp.clip(local_ids, 0, vocab_rows - 1), axis=0).astype(
        jnp.float32
    )
    picked = jnp.where(inside[:, :, None], picked, 0.0)
    summed = lax.psum(picked.astype(jnp.bfloat16), "section")
    embedded = lax.all_to_all(summed, "tp", split_axis=1, concat_axis=2, tiled=True)
    w_joint = jnp.concatenate([w_query[0], w_key[0], w_value[0]], axis=1)
    weight_local = jnp.max(jnp.abs(w_joint), axis=1).astype(jnp.float32)
    weight_peak = lax.pmax(weight_local.astype(jnp.bfloat16), "tp").astype(weight_local.dtype)
    w_out_local = w_out[0]
    out_peak = jnp.max(jnp.abs(w_out_local), axis=1).astype(jnp.float32)
    cosine, sine = rope_tables(length, HEAD_DIM)
    positions = jnp.arange(length, dtype=jnp.int32)
    causal = positions[:, None] >= positions[None, :]

    def project(portion):
        return jnp.dot(portion, w_joint, preferred_element_type=jnp.float32)

    def advance(clock, carry):
        incoming, stored, act_peak, head_peak = carry
        micro_index = clock - section_index
        active = (micro_index >= 0) & (micro_index < micros)
        slot_index = jnp.clip(micro_index, 0, micros - 1)
        arriving = lax.dynamic_index_in_dim(
            embedded, jnp.clip(clock, 0, micros - 1), 0, keepdims=False
        )
        resid = jnp.where(section_index == 0, arriving, incoming)
        normed = rms_normed(resid, gain_row)
        tick_peak = jnp.max(jnp.abs(normed), axis=0).astype(jnp.float32)
        joint = project(lax.all_gather(normed, "tp", axis=0, tiled=True))
        act_peak = jnp.where(active, jnp.maximum(act_peak, tick_peak), act_peak)
        query = joint[:, :query_cols]
        key_part = joint[:, query_cols : query_cols + kv_cols].astype(jnp.bfloat16)
        value_part = joint[:, query_cols + kv_cols :].astype(jnp.bfloat16)
        key_all, value_all = (
            lax.all_gather(key_part, "tp", axis=1, tiled=True),
            lax.all_gather(value_part, "tp", axis=1, tiled=True),
        )
        key_heads = jnp.einsum(
            "hg,kgd->khd",
            selector,
            key_all.reshape(length, KV_HEADS, HEAD_DIM),
            preferred_element_type=jnp.float32,
        )
        value_heads = jnp.einsum(
            "hg,kgd->khd",
            selector,
            value_all.reshape(length, KV_HEADS, HEAD_DIM),
            preferred_element_type=jnp.float32,
        ).astype(jnp.bfloat16)
        query_rot = rotate(query.reshape(length, heads_here, HEAD_DIM), cosine, sine).astype(
            jnp.bfloat16
        )
        key_rot = rotate(key_heads, cosine, sine).astype(jnp.bfloat16)
        scores = jnp.einsum(
            "qhd,khd->hqk", query_rot, key_rot, preferred_element_type=jnp.float32
        ) / math.sqrt(HEAD_DIM)
        scores = jnp.where(causal[None], scores, -1e30)
        probs = jax.nn.softmax(scores, axis=-1).astype(jnp.bfloat16)
        attended = jnp.einsum(
            "hqk,khd->qhd", probs, value_heads, preferred_element_type=jnp.float32
        )
        attended = attended.astype(jnp.bfloat16).reshape(length, query_cols)
        attended_peak = jnp.max(jnp.abs(attended), axis=0).astype(jnp.float32)
        head_peak = jnp.where(active, jnp.maximum(head_peak, attended_peak), head_peak)
        mixed = lax.psum_scatter(
            jnp.dot(attended, w_out_local, preferred_element_type=jnp.float32).astype(jnp.bfloat16),
            "tp",
            scatter_dimension=0,
            tiled=True,
        ).astype(jnp.float32)
        output = (resid.astype(jnp.float32) + mixed).astype(jnp.bfloat16)
        stored = jnp.where(
            active, lax.dynamic_update_index_in_dim(stored, output, slot_index, 0), stored
        )
        incoming = shifted(output, "section", 1)
        return (incoming, stored, act_peak, head_peak)

    width = embedded.shape[2]
    start_carry = (
        jnp.zeros((own_rows, width), jnp.bfloat16),
        jnp.zeros((micros, own_rows, width), jnp.bfloat16),
        jnp.zeros((width,), jnp.float32),
        jnp.zeros((query_cols,), jnp.float32),
    )
    incoming, stored, act_peak, head_peak = lax.fori_loop(
        0, micros + section_count - 1, advance, start_carry
    )
    act_peak = lax.pmax(act_peak.astype(jnp.bfloat16), "tp").astype(act_peak.dtype)
    alpha_exp = alpha_num[0].astype(jnp.float32) / 10.0
    scale_in = smoothing(act_peak, weight_peak, alpha_exp)
    scale_out = smoothing(head_peak, out_peak, alpha_exp)
    smoothed = (w_joint.astype(jnp.float32) * scale_in[:, None]).astype(jnp.bfloat16)
    smooth_query = smoothed[:, :query_cols]
    smooth_key = smoothed[:, query_cols : query_cols + kv_cols]
    smooth_value = smoothed[:, query_cols + kv_cols :]
    return (
        stored[None],
        scale_in[None],
        scale_out[None],
        smooth_query[None],
        smooth_key[None],
        smooth_value[None],
    )


def solution(mesh):
    return jax.shard_map(
        shards,
        mesh=mesh,
        in_specs=(
            P(),
            P(),
            P("section", "tp"),
            P("section", None),
            P("section", None, "tp"),
            P("section", None, "tp"),
            P("section", None, "tp"),
            P("section", "tp", None),
        ),
        out_specs=(
            P("section", None, "tp", None),
            P("section", None),
            P("section", "tp"),
            P("section", None, "tp"),
            P("section", None, "tp"),
            P("section", None, "tp"),
        ),
        check_vma=False,
    )
```

profile of v0, /device:TPU:5, one launch (start us, length us, event | category | flops | bytes accessed | tf_op | source)
XLA Modules:
  0.0 1146.5 jit_solution(14876491325339499638)
XLA Ops:
  9.0 9.1 gather_fusion
  18.1 2.0 select_convert_fusion
  20.1 5.0 abs_reduce_fusion.2
  25.2 1.1 copy.40
  26.3 2.7 copy.41
  29.7 22.9 %all-reduce.3.cloned.1.call-done = bf16[2,128,1024]{2,0,1:T(2,128)(2,1)} async-done(((bf16[2,128,1024]{2,0,1:T(2,128)(2,1)}), bf16[2,128,1024]{2,0,1:T(2,128)(2,1)}) %all-reduce.3.cloned.1.call-update) | async-done | bytes 524304 | tf_op jit(solution)/shard_map/psum | solution.py:76
  52.5 5.7 all-to-all-start
  58.2 11.4 abs_reduce_fusion.1
  69.6 2.0 all-to-all-done
  72.2 1014.4 %while.24 = (s32[]{:T(128)}, bf16[16,8192]{1,0:T(8,128)(2,1)S(1)}, bf16[2,16,8192]{2,1,0:T(8,128)(2,1)S(1)}, bf16[8192]{0:T(1024)(128)(2,1)S(1)}, f32[512]{0:T(5...) while((s32[]{:T(128)}, bf16[16,8192]{1,0:T(8,128)(2,1)S(1)}, ...), condition=%wide.region_8.9_spmd.clone.clone.clone.clone, body=%wide.region_1.0_spmd.clone.clone.clone.clone.sunk | while | flops 2455587072 | bytes 47066000 | solution.py:157
  72.5 0.9 abs_reduce_fusion.4
  73.8 49.7 %all-gather.2.cloned.1.call-done = bf16[128,8192]{1,0:T(8,128)(2,1)} async-done(((bf16[16,8192]{1,0:T(8,128)(2,1)}), bf16[128,8192]{1,0:T(8,128)(2,1)}) %all-gather.2.cloned.1.call-update) | async-done | bytes 2097168 | tf_op jit(solution)/shard_map/while/body/eval_jaxpr/all_gather | solution.py:101
  123.4 6.4 fusion.81
  130.0 24.2 %all_gather.40 = bf16[128,512]{0,1:T(8,128)(2,1)S(1)} all-gather(bf16[128,64]{0,1:T(8,128)(2,1)S(1)} %copy.66), channel_id=1, replica_groups=mesh['section'=4,'tp'=8] {'tp'}, dimensions={1}, use_global_device_ids=true | all-gather | bytes 147456 | tf_op jit(solution)/shard_map/while/body/eval_jaxpr/all_gather | solution.py:107
  155.9 24.3 %all_gather.41 = bf16[128,512]{0,1:T(8,128)(2,1)S(1)} all-gather(bf16[128,64]{0,1:T(8,128)(2,1)S(1)} %copy.68), channel_id=1, replica_groups=mesh['section'=4,'tp'=8] {'tp'}, dimensions={1}, use_global_device_ids=true | all-gather | bytes 147456 | tf_op jit(solution)/shard_map/while/body/eval_jaxpr/all_gather | solution.py:108
  181.0 6.0 convolution_convert_fusion.4
  187.0 80.0 %reduce-scatter.2.cloned.1.call-done = bf16[16,8192]{1,0:T(8,128)(2,1)} async-done(((bf16[128,8192]{1,0:T(8,128)(2,1)}), bf16[16,8192]{1,0:T(8,128)(2,1)}) %reduce-scatter.2.cloned.1.call-update) | async-done | bytes 262160 | tf_op jit(solution)/shard_map/while/body/eval_jaxpr/reduce_scatter | solution.py:137
  267.0 1.1 fusion.88
  268.0 1.3 collective-permute-start
  269.4 3.8 collective-permute-done
  273.4 0.9 abs_reduce_fusion.4
  274.7 52.0 %all-gather.2.cloned.1.call-done = bf16[128,8192]{1,0:T(8,128)(2,1)} async-done(((bf16[16,8192]{1,0:T(8,128)(2,1)}), bf16[128,8192]{1,0:T(8,128)(2,1)}) %all-gather.2.cloned.1.call-update) | async-done | bytes 2097168 | tf_op jit(solution)/shard_map/while/body/eval_jaxpr/all_gather | solution.py:101
  326.6 6.4 fusion.81
  333.2 24.2 %all_gather.40 = bf16[128,512]{0,1:T(8,128)(2,1)S(1)} all-gather(bf16[128,64]{0,1:T(8,128)(2,1)S(1)} %copy.66), channel_id=1, replica_groups=mesh['section'=4,'tp'=8] {'tp'}, dimensions={1}, use_global_device_ids=true | all-gather | bytes 147456 | tf_op jit(solution)/shard_map/while/body/eval_jaxpr/all_gather | solution.py:107
  359.2 24.3 %all_gather.41 = bf16[128,512]{0,1:T(8,128)(2,1)S(1)} all-gather(bf16[128,64]{0,1:T(8,128)(2,1)S(1)} %copy.68), channel_id=1, replica_groups=mesh['section'=4,'tp'=8] {'tp'}, dimensions={1}, use_global_device_ids=true | all-gather | bytes 147456 | tf_op jit(solution)/shard_map/while/body/eval_jaxpr/all_gather | solution.py:108
  384.2 6.0 convolution_convert_fusion.4
  390.2 80.1 %reduce-scatter.2.cloned.1.call-done = bf16[16,8192]{1,0:T(8,128)(2,1)} async-done(((bf16[128,8192]{1,0:T(8,128)(2,1)}), bf16[16,8192]{1,0:T(8,128)(2,1)}) %reduce-scatter.2.cloned.1.call-update) | async-done | bytes 262160 | tf_op jit(solution)/shard_map/while/body/eval_jaxpr/reduce_scatter | solution.py:137
  470.4 1.1 fusion.88
  471.4 1.3 collective-permute-start
  472.8 3.8 collective-permute-done
  478.1 51.9 %all-gather.2.cloned.1.call-done = bf16[128,8192]{1,0:T(8,128)(2,1)} async-done(((bf16[16,8192]{1,0:T(8,128)(2,1)}), bf16[128,8192]{1,0:T(8,128)(2,1)}) %all-gather.2.cloned.1.call-update) | async-done | bytes 2097168 | tf_op jit(solution)/shard_map/while/body/eval_jaxpr/all_gather | solution.py:101
  530.0 6.4 fusion.81
  536.6 24.2 %all_gather.40 = bf16[128,512]{0,1:T(8,128)(2,1)S(1)} all-gather(bf16[128,64]{0,1:T(8,128)(2,1)S(1)} %copy.66), channel_id=1, replica_groups=mesh['section'=4,'tp'=8] {'tp'}, dimensions={1}, use_global_device_ids=true | all-gather | bytes 147456 | tf_op jit(solution)/shard_map/while/body/eval_jaxpr/all_gather | solution.py:107
  562.6 24.3 %all_gather.41 = bf16[128,512]{0,1:T(8,128)(2,1)S(1)} all-gather(bf16[128,64]{0,1:T(8,128)(2,1)S(1)} %copy.68), channel_id=1, replica_groups=mesh['section'=4,'tp'=8] {'tp'}, dimensions={1}, use_global_device_ids=true | all-gather | bytes 147456 | tf_op jit(solution)/shard_map/while/body/eval_jaxpr/all_gather | solution.py:108
  587.6 6.0 convolution_convert_fusion.4
  593.6 80.0 %reduce-scatter.2.cloned.1.call-done = bf16[16,8192]{1,0:T(8,128)(2,1)} async-done(((bf16[128,8192]{1,0:T(8,128)(2,1)}), bf16[16,8192]{1,0:T(8,128)(2,1)}) %reduce-scatter.2.cloned.1.call-update) | async-done | bytes 262160 | tf_op jit(solution)/shard_map/while/body/eval_jaxpr/reduce_scatter | solution.py:137
  673.6 1.1 fusion.88
  674.6 1.3 collective-permute-start
  676.0 4.0 collective-permute-done
  681.5 52.1 %all-gather.2.cloned.1.call-done = bf16[128,8192]{1,0:T(8,128)(2,1)} async-done(((bf16[16,8192]{1,0:T(8,128)(2,1)}), bf16[128,8192]{1,0:T(8,128)(2,1)}) %all-gather.2.cloned.1.call-update) | async-done | bytes 2097168 | tf_op jit(solution)/shard_map/while/body/eval_jaxpr/all_gather | solution.py:101
  733.6 6.4 fusion.81
  740.2 24.2 %all_gather.40 = bf16[128,512]{0,1:T(8,128)(2,1)S(1)} all-gather(bf16[128,64]{0,1:T(8,128)(2,1)S(1)} %copy.66), channel_id=1, replica_groups=mesh['section'=4,'tp'=8] {'tp'}, dimensions={1}, use_global_device_ids=true | all-gather | bytes 147456 | tf_op jit(solution)/shard_map/while/body/eval_jaxpr/all_gather | solution.py:107
  766.1 24.3 %all_gather.41 = bf16[128,512]{0,1:T(8,128)(2,1)S(1)} all-gather(bf16[128,64]{0,1:T(8,128)(2,1)S(1)} %copy.68), channel_id=1, replica_groups=mesh['section'=4,'tp'=8] {'tp'}, dimensions={1}, use_global_device_ids=true | all-gather | bytes 147456 | tf_op jit(solution)/shard_map/while/body/eval_jaxpr/all_gather | solution.py:108
  791.2 6.0 convolution_convert_fusion.4
  797.2 80.0 %reduce-scatter.2.cloned.1.call-done = bf16[16,8192]{1,0:T(8,128)(2,1)} async-done(((bf16[128,8192]{1,0:T(8,128)(2,1)}), bf16[16,8192]{1,0:T(8,128)(2,1)}) %reduce-scatter.2.cloned.1.call-update) | async-done | bytes 262160 | tf_op jit(solution)/shard_map/while/body/eval_jaxpr/reduce_scatter | solution.py:137
  877.2 1.1 fusion.88
  878.2 1.3 collective-permute-start
  879.6 3.8 collective-permute-done
  884.9 51.9 %all-gather.2.cloned.1.call-done = bf16[128,8192]{1,0:T(8,128)(2,1)} async-done(((bf16[16,8192]{1,0:T(8,128)(2,1)}), bf16[128,8192]{1,0:T(8,128)(2,1)}) %all-gather.2.cloned.1.call-update) | async-done | bytes 2097168 | tf_op jit(solution)/shard_map/while/body/eval_jaxpr/all_gather | solution.py:101
  936.9 6.4 fusion.81
  943.5 24.2 %all_gather.40 = bf16[128,512]{0,1:T(8,128)(2,1)S(1)} all-gather(bf16[128,64]{0,1:T(8,128)(2,1)S(1)} %copy.66), channel_id=1, replica_groups=mesh['section'=4,'tp'=8] {'tp'}, dimensions={1}, use_global_device_ids=true | all-gather | bytes 147456 | tf_op jit(solution)/shard_map/while/body/eval_jaxpr/all_gather | solution.py:107
  969.4 24.3 %all_gather.41 = bf16[128,512]{0,1:T(8,128)(2,1)S(1)} all-gather(bf16[128,64]{0,1:T(8,128)(2,1)S(1)} %copy.68), channel_id=1, replica_groups=mesh['section'=4,'tp'=8] {'tp'}, dimensions={1}, use_global_device_ids=true | all-gather | bytes 147456 | tf_op jit(solution)/shard_map/while/body/eval_jaxpr/all_gather | solution.py:108
  994.4 6.0 convolution_convert_fusion.4
  1000.4 80.0 %reduce-scatter.2.cloned.1.call-done = bf16[16,8192]{1,0:T(8,128)(2,1)} async-done(((bf16[128,8192]{1,0:T(8,128)(2,1)}), bf16[16,8192]{1,0:T(8,128)(2,1)}) %reduce-scatter.2.cloned.1.call-update) | async-done | bytes 262160 | tf_op jit(solution)/shard_map/while/body/eval_jaxpr/reduce_scatter | solution.py:137
  1080.4 1.1 fusion.88
  1081.5 1.3 collective-permute-start
  1082.8 3.8 collective-permute-done
  1086.6 27.9 %all-reduce = (bf16[8192]{0:T(1024)(128)(2,1)S(1)}, bf16[8192]{0:T(1024)(128)(2,1)S(1)}) all-reduce(bf16[8192]{0:T(1024)(128)(2,1)S(1)} %get-tuple-element.540, bf16[8192]{0:T(1024)(128)(2,1)S(1)} %get-tuple-element.317), channel_id=1, replica_groups=mesh['section'=4,'tp'=8] {'tp'}, use_global_device_ids=true, to_apply=%region_11.12 | all-reduce | flops 16384 | bytes 65536 | tf_op jit(solution)/shard_map/pmax | solution.py:80
  1114.6 7.0 multiply_convert_fusion
  1121.6 4.0 copy-done
  1125.6 2.2 slice_bitcast_fusion.1
  1127.8 7.3 slice_bitcast_fusion
  1135.1 2.7 copy.42
  1137.8 1.6 copy.43
  (149 shorter events, 22.0 us)
Async XLA Ops:
  7.2 18.0 %copy-start.2 = (bf16[1,8192,64]{1,2,0:T(8,128)(2,1)S(1)}, bf16[1,8192,64]{1,2,0:T(8,128)(2,1)}, u32[]{:S(2)}) copy-start(bf16[1,8192,64]{1,2,0:T(8,128)(2,1)} %param.15) | copy-start | bytes 3145732
  7.2 45.4 %all-reduce.3.cloned.1.call-start = ((), (), s32[]{:S(2)}) async-start(), calls=%async_computation.2 | async-start | bytes 1048576 | tf_op jit(solution)/shard_map/psum | solution.py:76
  52.5 19.0 %all-to-all-start = ((bf16[2,128,1024]{2,0,1:T(2,128)(2,1)}), bf16[2,128,1024]{2,0,1:T(2,128)(2,1)S(1)}, u32[]{:S(2)}, u32[]{:S(2)}) async-start(bf16[2,128,1024]{2,0,1:T(2,128)(2,1)} %all-reduce.3.cloned.1.call-done), calls=%async_computation.1 | async-start | bytes 1048576 | tf_op jit(solution)/shard_map/all_to_all | solution.py:77
  58.2 14.0 %copy-start.3 = (f32[1,8192]{1,0:T(1,128)S(1)}, f32[1,8192]{1,0:T(1,128)}, u32[]{:S(2)}) copy-start(f32[1,8192]{1,0:T(1,128)} %param.13) | copy-start | bytes 98308
  72.2 51.2 %all-gather.2.cloned.1.call-start = ((), (), s32[]{:S(2)}) async-start(), calls=%async_computation.3 | async-start | bytes 2359296 | tf_op jit(solution)/shard_map/while/body/eval_jaxpr/all_gather | solution.py:101
  73.4 193.5 %reduce-scatter.2.cloned.1.call-start = ((), (), s32[]{:S(2)}) async-start(), calls=%async_computation.4 | async-start | bytes 2359296 | tf_op jit(solution)/shard_map/while/body/eval_jaxpr/reduce_scatter | solution.py:137
  268.0 5.1 collective-permute-start
  273.2 53.5 %all-gather.2.cloned.1.call-start = ((), (), s32[]{:S(2)}) async-start(), calls=%async_computation.3 | async-start | bytes 2359296 | tf_op jit(solution)/shard_map/while/body/eval_jaxpr/all_gather | solution.py:101
  274.3 196.0 %reduce-scatter.2.cloned.1.call-start = ((), (), s32[]{:S(2)}) async-start(), calls=%async_computation.4 | async-start | bytes 2359296 | tf_op jit(solution)/shard_map/while/body/eval_jaxpr/reduce_scatter | solution.py:137
  471.4 5.2 collective-permute-start
  476.6 53.4 %all-gather.2.cloned.1.call-start = ((), (), s32[]{:S(2)}) async-start(), calls=%async_computation.3 | async-start | bytes 2359296 | tf_op jit(solution)/shard_map/while/body/eval_jaxpr/all_gather | solution.py:101
  477.8 195.8 %reduce-scatter.2.cloned.1.call-start = ((), (), s32[]{:S(2)}) async-start(), calls=%async_computation.4 | async-start | bytes 2359296 | tf_op jit(solution)/shard_map/while/body/eval_jaxpr/reduce_scatter | solution.py:137
  674.6 5.3 collective-permute-start
  680.0 53.6 %all-gather.2.cloned.1.call-start = ((), (), s32[]{:S(2)}) async-start(), calls=%async_computation.3 | async-start | bytes 2359296 | tf_op jit(solution)/shard_map/while/body/eval_jaxpr/all_gather | solution.py:101
  681.2 196.0 %reduce-scatter.2.cloned.1.call-start = ((), (), s32[]{:S(2)}) async-start(), calls=%async_computation.4 | async-start | bytes 2359296 | tf_op jit(solution)/shard_map/while/body/eval_jaxpr/reduce_scatter | solution.py:137
  878.2 5.2 collective-permute-start
  883.4 53.5 %all-gather.2.cloned.1.call-start = ((), (), s32[]{:S(2)}) async-start(), calls=%async_computation.3 | async-start | bytes 2359296 | tf_op jit(solution)/shard_map/while/body/eval_jaxpr/all_gather | solution.py:101
  884.6 195.8 %reduce-scatter.2.cloned.1.call-start = ((), (), s32[]{:S(2)}) async-start(), calls=%async_computation.4 | async-start | bytes 2359296 | tf_op jit(solution)/shard_map/while/body/eval_jaxpr/reduce_scatter | solution.py:137
  1081.5 5.1 collective-permute-start
  1086.6 35.0 %copy-start.1 = (bf16[2,16,8192]{2,1,0:T(8,128)(2,1)}, bf16[2,16,8192]{2,1,0:T(8,128)(2,1)S(1)}, u32[]{:S(2)}) copy-start(bf16[2,16,8192]{2,1,0:T(8,128)(2,1)S(1)} %get-tuple-element.316) | copy-start | bytes 1572868
  1114.5 7.0 copy-start.4
  1121.6 4.0 copy-start
Sparse Core Ops, SparseCore 0:
  20.2 32.2 all-reduce.2
  75.7 47.6 all-gather.1
  187.1 79.7 reduce-scatter.1
  276.4 50.2 all-gather.1
  390.3 79.9 reduce-scatter.1
  479.8 50.2 all-gather.1
  593.7 79.7 reduce-scatter.1
  683.5 50.0 all-gather.1
  797.3 79.8 reduce-scatter.1
  886.6 50.2 all-gather.1
  1000.5 79.8 reduce-scatter.1
where the time goes:
time: 1160 us; the launch traced here: 1150 us
  waiting for transfers between devices  702 us (61%)
  blocking collectives  270 us (23%)
  matrix products  67.6 us (6%)
  other arithmetic  44.4 us (4%)
  local copies, waits for them, and re-layouts  34.9 us (3%)
  between operations  14.5 us (1%)
  starting transfers between devices  12.4 us (1%)
    reduce_scatter x5, waiting for transfers between devices, advance(): lax.psum_scatter(jnp.dot(attended, w_out_local, preferred_element_type=jn...  400 us
    all_gather x5, waiting for transfers between devices, advance(): joint = project(lax.all_gather(normed, 'tp', axis=0, tiled=True))  258 us
    all_gather x5, blocking collectives, advance(): lax.all_gather(value_part, 'tp', axis=1, tiled=True)  121 us
    all_gather x5, blocking collectives, advance(): lax.all_gather(key_part, 'tp', axis=1, tiled=True)  121 us
    dot_general x5, matrix products, project(): return jnp.dot(portion, w_joint, preferred_element_type=jnp.float32)  32.1 us
    dot_general x5, matrix products, advance(): jnp.dot(attended, w_out_local, preferred_element_type=jnp.float32)  30.1 us
    pmax x1, blocking collectives, shards(): lax.pmax(weight_local.astype(jnp.bfloat16), 'tp').astype(weight_local.dtype)  27.9 us
  transfers between devices with their start and end apart: 17, of which 17 were waited for; matrix products, arithmetic and copies ran while one was open for 2% of the time, Pallas kernels for 0%

commit v1 on v0

v1 whole, which is shorter than its diff:
```python
import functools
import math

import jax
import jax.numpy as jnp
from jax import lax
from jax.experimental import pallas as pl
from jax.experimental.pallas import tpu as pltpu
from jax.sharding import PartitionSpec as P

KV_HEADS = 4
HEAD_DIM = 128


norm_eps = 1e-05
stat_eps = 1e-05
rope_base = 500000.0


def rope_tables(length, head_size):
    halves = head_size // 2
    freqs = jnp.exp(-math.log(rope_base) * 2.0 * jnp.arange(halves, dtype=jnp.float32) / head_size)
    angles = jnp.arange(length, dtype=jnp.float32)[:, None] * freqs[None, :]
    return (jnp.cos(angles), jnp.sin(angles))


def smoothing(act_peak, weight_peak, alpha_exp):
    return jnp.exp(
        alpha_exp * jnp.log(act_peak + stat_eps)
        - (1.0 - alpha_exp) * jnp.log(weight_peak + stat_eps)
    )


MESH = pl.DeviceIdType.MESH
CHUNKS = 2
TILE = 512


def remote(src, dst, send, recv, where):
    return pltpu.make_async_remote_copy(
        src_ref=src, dst_ref=dst, send_sem=send, recv_sem=recv, device_id=where, device_id_type=MESH
    )


def grid_of(count):
    minor = 1
    while (2 * minor) * (2 * minor) <= count and count % (2 * minor) == 0:
        minor *= 2
    return (count // minor, minor)


def layers_kernel(
    sections,
    count,
    embedded,
    gain,
    wq_hbm,
    wkv_hbm,
    wo_hbm,
    cos2,
    sin2,
    wpeak_in,
    out,
    act_out,
    head_out,
    wpeak_out,
    wq,
    wkv,
    wo,
    xin,
    ag,
    acc_q,
    acc_kv,
    kvbuf,
    krot,
    vall,
    att,
    part,
    r1,
    s2,
    r2,
    own,
    wpbuf,
    load_sem,
    xin_r,
    xin_s,
    ag_s,
    ag_f,
    ag_r,
    kv_s,
    kv_r,
    r1_s,
    r1_r,
    s2_s,
    r2_r,
    wp_s,
    wp_r,
):
    major, minor = grid_of(count)
    section = lax.axis_index("section")
    me = lax.axis_index("tp")
    a = me // minor
    b = me % minor
    micros, rows, width = embedded.shape
    length = rows * count
    query_cols = wq.shape[1]
    kv_cols = wkv.shape[1] // 2
    heads_here = query_cols // HEAD_DIM
    per_head = HEAD_DIM // kv_cols
    span = width // CHUNKS
    loads = [
        pltpu.make_async_copy(wq_hbm, wq, load_sem.at[0]),
        pltpu.make_async_copy(wkv_hbm, wkv, load_sem.at[1]),
        pltpu.make_async_copy(wo_hbm, wo, load_sem.at[2]),
    ]
    for load in loads:
        load.start()

    def peer(number):
        return (section, number)

    def col_peer(step):
        return lax.rem(a + step + major, major)

    def row_peer(step):
        return lax.rem(b + step + minor, minor)

    barrier = pltpu.get_barrier_semaphore()
    for step in range(1, count):
        pl.semaphore_signal(
            barrier, inc=1, device_id=peer(lax.rem(me + step, count)), device_id_type=MESH
        )

    @pl.when(section > 0)
    def _():
        pl.semaphore_signal(barrier, inc=1, device_id=(section - 1, me), device_id_type=MESH)

    @pl.when(section < sections - 1)
    def _():
        pl.semaphore_signal(barrier, inc=1, device_id=(section + 1, me), device_id_type=MESH)

    before = (section + sections - 1) // sections
    after = (2 * sections - 2 - section) // sections
    pl.semaphore_wait(barrier, count - 1 + before + after)

    act_out[...] = jnp.zeros_like(act_out)
    head_out[...] = jnp.zeros_like(head_out)
    positions = lax.broadcasted_iota(jnp.int32, (length, length), 0)
    keys_at = lax.broadcasted_iota(jnp.int32, (length, length), 1)
    causal = positions >= keys_at

    def weight_copy(step):
        return remote(
            wpeak_in,
            wpbuf.at[me],
            wp_s.at[step - 1],
            wp_r.at[me],
            peer(lax.rem(me + step, count)),
        )

    def rotated(values):
        turned = pltpu.roll(values, HEAD_DIM // 2, 1)
        return (values * cos2[...] + turned * sin2[...]).astype(jnp.bfloat16)

    def tile_at(index):
        return pl.ds(pl.multiple_of(index * TILE, TILE), TILE)

    def micro_step(m, first):
        @pl.when(section == 0)
        def _():
            xin[m] = embedded[m]

        @pl.when(section > 0)
        def _():
            remote(
                xin.at[m], xin.at[m], xin_s.at[0], xin_r.at[m], (section - 1, me)
            ).wait_recv()

        def square(index, total):
            values = xin[m, :, tile_at(index)].astype(jnp.float32)
            return total + jnp.sum(values * values, axis=1, keepdims=True)

        total = lax.fori_loop(
            0, width // TILE, square, jnp.zeros((rows, 1), jnp.float32), unroll=True
        )
        inverse = lax.rsqrt(total / width + norm_eps)
        for index in range(width // TILE):
            cols = pl.ds(index * TILE, TILE)
            values = xin[m, :, cols].astype(jnp.float32)
            ag[m, me, :, cols] = (values * inverse * gain[:, cols]).astype(jnp.bfloat16)

        def column_copy(step):
            return remote(
                ag.at[m, me],
                ag.at[m, me],
                ag_s.at[step - 1],
                ag_r.at[m, me],
                peer(col_peer(step) * minor + b),
            )

        def row_copy(origin, order, step):
            return remote(
                ag.at[m, origin],
                ag.at[m, origin],
                ag_f.at[order, step - 1],
                ag_r.at[m, origin],
                peer(a * minor + row_peer(step)),
            )

        for step in range(1, major):
            column_copy(step).start()
        for step in range(1, minor):
            row_copy(me, 0, step).start()
        for order in range(1, major):
            origin = col_peer(-order) * minor + b
            row_copy(origin, order, 1).wait_recv()
            for step in range(1, minor):
                row_copy(origin, order, step).start()
        for order in range(major):
            for step in range(1, minor):
                origin = col_peer(-order) * minor + row_peer(step)
                row_copy(origin, order, step).wait_recv()

        @pl.when(first)
        def _():
            for load in loads:
                load.wait()
            for step in range(1, count):
                weight_copy(step).start()

        acc_q[...] = jnp.zeros_like(acc_q)
        acc_kv[...] = jnp.zeros_like(acc_kv)

        @pl.loop(0, width // TILE)
        def _(index):
            cols = tile_at(index)
            if rows % 16 == 0:
                normed = ag[m, :, :, cols].reshape(length, TILE)
            else:
                wide = ag[m, :, :, cols].astype(jnp.float32)
                normed = wide.reshape(length, TILE).astype(jnp.bfloat16)
            acc_q[...] += jnp.dot(normed, wq[cols, :], preferred_element_type=jnp.float32)
            acc_kv[...] += jnp.dot(normed, wkv[cols, :], preferred_element_type=jnp.float32)
            peak = jnp.max(jnp.abs(normed.astype(jnp.float32)), axis=0, keepdims=True)
            act_out[:, cols] = jnp.maximum(act_out[:, cols], peak)

        kvbuf[m, me] = acc_kv[...].astype(jnp.bfloat16)

        def kv_copy(step):
            return remote(
                kvbuf.at[m, me],
                kvbuf.at[m, me],
                kv_s.at[step - 1],
                kv_r.at[m, me],
                peer(lax.rem(me + step, count)),
            )

        for step in range(1, count):
            kv_copy(step).start()
        queries = [
            rotated(acc_q[:, head * HEAD_DIM : (head + 1) * HEAD_DIM])
            for head in range(heads_here)
        ]
        for step in range(1, count):
            origin = lax.rem(me - step + count, count)
            remote(
                kvbuf.at[m, origin],
                kvbuf.at[m, origin],
                kv_s.at[step - 1],
                kv_r.at[m, origin],
                peer(origin),
            ).wait_recv()
        for group in range(KV_HEADS):
            blocks = [
                kvbuf[m, group * per_head + piece].astype(jnp.float32) for piece in range(per_head)
            ]
            key = jnp.concatenate([block[:, :kv_cols] for block in blocks], axis=1)
            value = jnp.concatenate([block[:, kv_cols:] for block in blocks], axis=1)
            krot[group] = rotated(key)
            vall[group] = value.astype(jnp.bfloat16)
        for head in range(heads_here):
            if heads_here % KV_HEADS == 0:
                group = head % KV_HEADS
            else:
                group = lax.rem(me * heads_here + head, KV_HEADS)
            scores = lax.dot_general(
                queries[head],
                krot[group],
                (((1,), (1,)), ((), ())),
                preferred_element_type=jnp.float32,
            ) / math.sqrt(HEAD_DIM)
            scores = jnp.where(causal, scores, -1e30)
            weights = jnp.exp(scores - jnp.max(scores, axis=1, keepdims=True))
            probs = (weights / jnp.sum(weights, axis=1, keepdims=True)).astype(jnp.bfloat16)
            mixed = jnp.dot(probs, vall[group], preferred_element_type=jnp.float32)
            mixed = mixed.astype(jnp.bfloat16)
            cols = pl.ds(head * HEAD_DIM, HEAD_DIM)
            att[:, cols] = mixed
            peak = jnp.max(jnp.abs(mixed.astype(jnp.float32)), axis=0, keepdims=True)
            head_out[:, cols] = jnp.maximum(head_out[:, cols], peak)

        orders = list(range(1, major)) + [0]

        def first_copy(chunk, step, order):
            other_b = row_peer(step)
            other_a = col_peer(order)
            return remote(
                part.at[chunk, other_b, other_a],
                r1.at[m, chunk, b, other_a],
                r1_s.at[chunk, step - 1, order],
                r1_r.at[m, chunk, b, other_a],
                peer(a * minor + other_b),
            )

        def second_copy(chunk, order):
            return remote(
                s2.at[chunk, order - 1],
                r2.at[m, chunk, a],
                s2_s.at[chunk, order - 1],
                r2_r.at[m, chunk, a],
                peer(col_peer(order) * minor + b),
            )

        for chunk in range(CHUNKS):

            @pl.loop(0, span // TILE)
            def _(index):
                cols = tile_at(index)
                source = tile_at(index + chunk * (span // TILE))
                product = jnp.dot(att[...], wo[:, source], preferred_element_type=jnp.float32)
                for i in range(major):
                    for j in range(minor):
                        top = (i * minor + j) * rows
                        part[chunk, j, i, :, cols] = product[top : top + rows].astype(jnp.bfloat16)

            for order in orders:
                for step in range(1, minor):
                    first_copy(chunk, step, order).start()
        for chunk in range(CHUNKS):
            for order in orders:
                other_a = col_peer(order)
                for step in range(1, minor):
                    origin = row_peer(step)
                    remote(
                        r1.at[m, chunk, origin, other_a],
                        r1.at[m, chunk, origin, other_a],
                        r1_s.at[chunk, step - 1, order],
                        r1_r.at[m, chunk, origin, other_a],
                        peer(a * minor + origin),
                    ).wait_recv()
                for index in range(span // TILE):
                    cols = pl.ds(index * TILE, TILE)
                    total = part[chunk, b, other_a, :, cols].astype(jnp.float32)
                    for step in range(1, minor):
                        total += r1[m, chunk, row_peer(step), other_a, :, cols].astype(jnp.float32)
                    if order == 0:
                        own[chunk, :, cols] = total
                    else:
                        s2[chunk, order - 1, :, cols] = total.astype(jnp.bfloat16)
                if order != 0:
                    second_copy(chunk, order).start()
        for chunk in range(CHUNKS):
            for order in range(1, major):
                origin = col_peer(-order)
                remote(
                    r2.at[m, chunk, origin],
                    r2.at[m, chunk, origin],
                    s2_s.at[chunk, order - 1],
                    r2_r.at[m, chunk, origin],
                    peer(origin * minor + b),
                ).wait_recv()
            for index in range(span // TILE):
                cols = pl.ds(index * TILE, TILE)
                full = pl.ds(chunk * span + index * TILE, TILE)
                total = own[chunk, :, cols]
                for order in range(1, major):
                    total += r2[m, chunk, col_peer(-order), :, cols].astype(jnp.float32)
                out[m, :, full] = (xin[m, :, full].astype(jnp.float32) + total).astype(jnp.bfloat16)

        def onward():
            return remote(
                out.at[m], xin.at[m], xin_s.at[0], xin_r.at[m], (section + 1, me)
            )

        @pl.when(section < sections - 1)
        def _():
            onward().start()

        for step in range(1, major):
            column_copy(step).wait_send()
        for order in range(major):
            for step in range(1, minor):
                row_copy(col_peer(-order) * minor + b, order, step).wait_send()
        for step in range(1, count):
            kv_copy(step).wait_send()
        for chunk in range(CHUNKS):
            for order in orders:
                for step in range(1, minor):
                    first_copy(chunk, step, order).wait_send()
                if order != 0:
                    second_copy(chunk, order).wait_send()

        @pl.when(section < sections - 1)
        def _():
            onward().wait_send()

    @pl.loop(0, micros)
    def _(m):
        micro_step(m, m == 0)

    peak = wpeak_in[...]
    for step in range(1, count):
        origin = lax.rem(me + step, count)
        remote(
            wpeak_in, wpbuf.at[origin], wp_s.at[step - 1], wp_r.at[origin], peer(origin)
        ).wait_recv()
        peak = jnp.maximum(peak, wpbuf[origin])
    wpeak_out[...] = peak
    for step in range(1, count):
        weight_copy(step).wait_send()


def run_layers(sections, count, embedded, gain, wq, wkv, wo, cos2, sin2, wpeak):
    major, minor = grid_of(count)
    micros, rows, width = embedded.shape
    length = rows * count
    query_cols = wq.shape[1]
    kv_two = wkv.shape[1]
    span = width // CHUNKS
    bf16, f32 = jnp.bfloat16, jnp.float32
    vmem = pl.BlockSpec(memory_space=pltpu.VMEM)
    anywhere = pl.BlockSpec(memory_space=pl.ANY)
    dma = pltpu.SemaphoreType.DMA
    return pl.pallas_call(
        functools.partial(layers_kernel, sections, count),
        out_shape=(
            jax.ShapeDtypeStruct((micros, rows, width), bf16),
            jax.ShapeDtypeStruct((1, width), f32),
            jax.ShapeDtypeStruct((1, query_cols), f32),
            jax.ShapeDtypeStruct(wpeak.shape, f32),
        ),
        in_specs=[vmem, vmem, anywhere, anywhere, anywhere, vmem, vmem, vmem],
        out_specs=(vmem, vmem, vmem, vmem),
        scratch_shapes=[
            pltpu.VMEM(wq.shape, bf16),
            pltpu.VMEM(wkv.shape, bf16),
            pltpu.VMEM(wo.shape, bf16),
            pltpu.VMEM((micros, rows, width), bf16),
            pltpu.VMEM((micros, count, rows, width), bf16),
            pltpu.VMEM((length, query_cols), f32),
            pltpu.VMEM((length, kv_two), f32),
            pltpu.VMEM((micros, count, length, kv_two), bf16),
            pltpu.VMEM((KV_HEADS, length, HEAD_DIM), bf16),
            pltpu.VMEM((KV_HEADS, length, HEAD_DIM), bf16),
            pltpu.VMEM((length, query_cols), bf16),
            pltpu.VMEM((CHUNKS, minor, major, rows, span), bf16),
            pltpu.VMEM((micros, CHUNKS, minor, major, rows, span), bf16),
            pltpu.VMEM((CHUNKS, major - 1, rows, span), bf16),
            pltpu.VMEM((micros, CHUNKS, major, rows, span), bf16),
            pltpu.VMEM((CHUNKS, rows, span), f32),
            pltpu.VMEM((count,) + wpeak.shape, f32),
            dma((3,)),
            dma((micros,)),
            dma((1,)),
            dma((major - 1,)),
            dma((major, minor - 1)),
            dma((micros, count)),
            dma((count - 1,)),
            dma((micros, count)),
            dma((CHUNKS, minor - 1, major)),
            dma((micros, CHUNKS, minor, major)),
            dma((CHUNKS, major - 1)),
            dma((micros, CHUNKS, major)),
            dma((count - 1,)),
            dma((count,)),
        ],
        compiler_params=pltpu.CompilerParams(
            collective_id=0, has_side_effects=True, vmem_limit_bytes=60 * 1024 * 1024
        ),
        name="layers",
    )(embedded, gain, wq, wkv, wo, cos2, sin2, wpeak)


def shards(token_ids, alpha_num, embed_table, norm_gain, w_query, w_key, w_value, w_out):
    tp_count = lax.axis_size("tp")
    section_count = lax.axis_size("section")
    section_index = lax.axis_index("section")
    length = token_ids.shape[1]
    vocab_rows = embed_table.shape[0]
    local_ids = token_ids - section_index * vocab_rows
    inside = (local_ids >= 0) & (local_ids < vocab_rows)
    picked = jnp.take(embed_table, jnp.clip(local_ids, 0, vocab_rows - 1), axis=0)
    picked = jnp.where(inside[:, :, None], picked, jnp.zeros_like(picked))
    summed = lax.psum(picked, "section")
    embedded = lax.all_to_all(summed, "tp", split_axis=1, concat_axis=2, tiled=True)
    w_query, w_key, w_value, w_out = w_query[0], w_key[0], w_value[0], w_out[0]
    w_kv = jnp.concatenate([w_key, w_value], axis=1)
    weight_local = jnp.maximum(
        jnp.max(jnp.abs(w_query), axis=1), jnp.max(jnp.abs(w_kv), axis=1)
    ).astype(jnp.float32)
    out_peak = jnp.max(jnp.abs(w_out), axis=1).astype(jnp.float32)
    cosine, sine = rope_tables(length, HEAD_DIM)
    cos2 = jnp.concatenate([cosine, cosine], axis=1)
    sin2 = jnp.concatenate([-sine, sine], axis=1)
    stored, act_peak, head_peak, weight_peak = run_layers(
        section_count,
        tp_count,
        embedded,
        norm_gain,
        w_query,
        w_kv,
        w_out,
        cos2,
        sin2,
        weight_local.reshape(-1, 128),
    )
    alpha_exp = alpha_num[0].astype(jnp.float32) / 10.0
    scale_in = smoothing(act_peak[0], weight_peak.reshape(-1), alpha_exp)
    scale_out = smoothing(head_peak[0], out_peak, alpha_exp)

    def smoothed(weights):
        return (weights.astype(jnp.float32) * scale_in[:, None]).astype(jnp.bfloat16)

    return (
        stored[None],
        scale_in[None],
        scale_out[None],
        smoothed(w_query)[None],
        smoothed(w_key)[None],
        smoothed(w_value)[None],
    )


def solution(mesh):
    return jax.shard_map(
        shards,
        mesh=mesh,
        in_specs=(
            P(),
            P(),
            P("section", "tp"),
            P("section", None),
            P("section", None, "tp"),
            P("section", None, "tp"),
            P("section", None, "tp"),
            P("section", "tp", None),
        ),
        out_specs=(
            P("section", None, "tp", None),
            P("section", None),
            P("section", "tp"),
            P("section", None, "tp"),
            P("section", None, "tp"),
            P("section", None, "tp"),
        ),
        check_vma=False,
    )
```

time: 1160 us -> 418 us (0.36); the launches traced: 1150 us -> 417 us
  waiting for transfers between devices: 702 us -> 25 us
  Pallas kernels: 0 us -> 324 us
  blocking collectives: 270 us -> 0 us
  matrix products: 67.6 us -> 0 us
  local copies, waits for them, and re-layouts: 34.9 us -> 15.2 us
  other arithmetic: 44.4 us -> 31.9 us
    reduce_scatter x5 -> x0, waiting for transfers between devices: 400 us -> none  [advance(): lax.psum_scatter(jnp.dot(attended, w_out_local, preferred_element_type=jn...]
    pallas_call x0 -> x1, Pallas kernels: none -> 324 us  [run_layers(): pl.pallas_call(functools.partial(layers_kernel, sections, count), out_sha...]
    all_gather x5 -> x0, waiting for transfers between devices: 258 us -> none  [advance(): joint = project(lax.all_gather(normed, 'tp', axis=0, tiled=True))]
    all_gather x10 -> x0, blocking collectives: 242 us -> none  [the longest x5 121 us: advance(): lax.all_gather(value_part, 'tp', axis=1, tiled=True)]
    dot_general x30 -> x0, matrix products: 67.6 us -> none  [the longest x5 32.1 us: project(): return jnp.dot(portion, w_joint, preferred_element_type=jnp.float32)]
    pmax x1 -> x0, blocking collectives: 27.9 us -> none  [shards(): lax.pmax(weight_local.astype(jnp.bfloat16), 'tp').astype(weight_local.dtype)]
    ppermute x5 -> x0, waiting for transfers between devices: 19.2 us -> none  [shifted(): lax.ppermute(value, axis, [(source, source + steps) for source in range(f...]
  transfers between devices with their start and end apart: 17 -> 2, of which waited for: 17 -> 2; matrix products, arithmetic and copies ran while one was open for 2% -> 5% of each run, Pallas kernels for 0% -> 0%
where the time goes in v1:
time: 418 us; the launch traced here: 417 us
  Pallas kernels  324 us (78%)
  other arithmetic  31.9 us (8%)
  waiting for transfers between devices  25 us (6%)
  local copies, waits for them, and re-layouts  15.2 us (4%)
  between operations  14.8 us (4%)
  starting transfers between devices  5.71 us (1%)
    pallas_call x1, Pallas kernels, run_layers(): pl.pallas_call(functools.partial(layers_kernel, sections, count), out_sha...  324 us
    psum x1, waiting for transfers between devices, shards(): summed = lax.psum(picked, 'section')  18.3 us
    convert_element_type x2, other arithmetic, smoothed(): (weights.astype(jnp.float32) * scale_in[:, None]).astype(jnp.bfloat16)  9.44 us
    gather x1, local copies, waits for them, and re-layouts, shards(): jnp.take(embed_table, jnp.clip(local_ids, 0, vocab_rows - 1), axis=0)  9.39 us
  transfers between devices with their start and end apart: 2, of which 2 were waited for; matrix products, arithmetic and copies ran while one was open for 5% of the time, Pallas kernels for 0%

profile of v1, /device:TPU:5, one launch (start us, length us, event | category | flops | bytes accessed | tf_op | source)
XLA Modules:
  0.0 417.0 jit_solution(13938724951861452269)
XLA Ops:
  7.2 0.0 all-reduce.2.cloned.1.call-start
  7.2 0.7 fusion.4
  7.9 0.7 compare_and_fusion
  8.6 0.1 copy.20
  8.7 0.1 copy.19
  8.9 9.4 %gather_fusion = bf16[256,1024]{1,0:T(8,128)(2,1)S(1)} fusion(bf16[16384,1024]{1,0:T(8,128)(2,1)} %param.10, s32[1024]{0:T(1024)S(1)} %pad_clamp_fusion), kind=kCustom, calls=%fused_computation | custom fusion | bytes 1049600 | tf_op jit(solution)/shard_map/jit(_take)/gather | solution.py:492
  18.3 1.9 broadcast_select_fusion.1
  20.2 0.0 all-reduce.2.cloned.1.call-update
  20.8 0.0 copy-start
  20.8 5.1 %abs_reduce_fusion = bf16[512]{0:T(512)(128)(2,1)S(1)} fusion(bf16[1,512,8192]{2,1,0:T(8,128)(2,1)} %param.15), kind=kLoop, calls=%fused_computation.2 | loop fusion | flops 8388096 | bytes 8389632 | tf_op jit(solution)/shard_map/reduce_max | solution.py:501
  26.0 2.0 copy.24
  28.0 0.0 copy-done
  28.0 1.8 copy.25
  29.8 4.2 %abs_reduce_fusion.2 = (bf16[8192]{0:T(1024)(128)(2,1)S(1)}, bf16[8192,128]{1,0:T(8,128)(2,1)}) fusion(bf16[8192,64]{1,0:T(8,128)(2,1)} %bitcast.29, bf16[8192,64]{1,0:T(8,128)(2,1)S(1)} %bitcast.28), kind=kLoop, calls=%fused_computation.7 | loop fusion | flops 7331840 | bytes 4210688 | tf_op jit(solution)/shard_map/reduce_max | solution.py:499
  34.0 0.3 fusion.3
  34.3 18.3 %all-reduce.2.cloned.1.call-done = bf16[2,128,1024]{2,0,1:T(2,128)(2,1)} async-done(((bf16[2,128,1024]{2,0,1:T(2,128)(2,1)}), bf16[2,128,1024]{2,0,1:T(2,128)(2,1)}) %all-reduce.2.cloned.1.call-update) | async-done | bytes 524304 | tf_op jit(solution)/shard_map/psum | solution.py:494
  52.6 5.7 %all-to-all-start = ((bf16[2,128,1024]{2,0,1:T(2,128)(2,1)}), bf16[2,128,1024]{2,0,1:T(2,128)(2,1)S(1)}, u32[]{:S(2)}, u32[]{:S(2)}) async-start(bf16[2,128,1024]{2,0,1:T(2,128)(2,1)} %all-reduce.2.cloned.1.call-done), calls=%async_computation | async-start | bytes 1048576 | tf_op jit(solution)/shard_map/all_to_all | solution.py:495
  58.3 0.8 pad_maximum_fusion.1
  59.0 5.3 %abs_reduce_fusion.1 = bf16[8192]{0:T(1024)(128)(2,1)S(1)} fusion(bf16[1,8192,512]{2,1,0:T(8,128)(2,1)} %param.12), kind=kLoop, calls=%fused_computation.3 | loop fusion | flops 8380416 | bytes 8404992 | tf_op jit(solution)/shard_map/reduce_max | solution.py:499
  64.3 0.6 bitcast_convert_fusion.wpeak_in
  64.9 6.7 %all-to-all-done = bf16[2,128,1024]{2,0,1:T(2,128)(2,1)S(1)} async-done(((bf16[2,128,1024]{2,0,1:T(2,128)(2,1)}), bf16[2,128,1024]{2,0,1:T(2,128)(2,1)S(1)}, u32[]{:S(2)}, u32[]{:S(2)}) %all-to-all-start) | async-done | bytes 524320 | tf_op jit(solution)/shard_map/all_to_all | solution.py:495
  71.6 0.1 copy.22
  71.7 0.8 copy.26
  72.6 0.0 copy-start.1
  72.6 324.4 %layers.1 = (bf16[2,16,8192]{2,1,0:T(8,128)(2,1)}, f32[1,8192]{1,0:T(1,128)}, f32[1,512]{1,0:T(1,128)}, f32[64,128]{1,0:T(8,128)}) custom-call(bf16[2,16,8192]{2,1,0:T(8,128)(2,1)} %bitcast.30, f32[1,8192]{1,0:T(1,128)} %gain.1, bf16[8192,512]{1,0:T(8,128)(2,1)} %bitcast.26, bf16[8192,128]{1,0:T(8,128)(2,1)} %get-tuple-element.17.wkv_hbm, ...), custom_call_target="tpu_custom_call" | custom-call | tf_op jit(solution)/shard_map/layers/pallas_call | solution.py:434
  397.0 0.8 log_multiply_fusion.1
  397.8 0.8 fusion.2
  398.6 0.0 copy-done.1
  398.6 1.7 multiply_convert_fusion.1
  400.3 0.0 copy-start.3
  400.3 0.0 copy-start.4
  400.3 0.0 copy-start.2
  400.3 7.7 %multiply_convert_fusion = bf16[1,8192,512]{2,1,0:T(8,128)(2,1)} fusion(bf16[1,8192,512]{2,1,0:T(8,128)(2,1)} %param.12, f32[8192]{0:T(1024)S(1)} %get-tuple-element.14), kind=kLoop, calls=%fused_computation.1 | loop fusion | flops 12582912 | bytes 16809984 | tf_op jit(solution)/shard_map/convert_element_type | solution.py:522
  408.0 0.0 copy-done.3
  408.0 0.7 subtract_exponential_fusion
  408.7 0.0 copy-done.4
  408.7 0.6 subtract_exponential_fusion.1
  409.3 0.0 copy-done.2
  409.3 0.8 copy.31
  (3 shorter events, 0.0 us)
Async XLA Ops:
  7.2 45.4 %all-reduce.2.cloned.1.call-start = ((), (), s32[]{:S(2)}) async-start(), calls=%async_computation.1 | async-start | bytes 1048576 | tf_op jit(solution)/shard_map/psum | solution.py:494
  20.8 7.2 %copy-start = (bf16[1,8192,64]{1,2,0:T(8,128)(2,1)S(1)}, bf16[1,8192,64]{1,2,0:T(8,128)(2,1)}, u32[]{:S(2)}) copy-start(bf16[1,8192,64]{1,2,0:T(8,128)(2,1)} %param.14) | copy-start | bytes 3145732
  52.6 19.0 %all-to-all-start = ((bf16[2,128,1024]{2,0,1:T(2,128)(2,1)}), bf16[2,128,1024]{2,0,1:T(2,128)(2,1)S(1)}, u32[]{:S(2)}, u32[]{:S(2)}) async-start(bf16[2,128,1024]{2,0,1:T(2,128)(2,1)} %all-reduce.2.cloned.1.call-done), calls=%async_computation | async-start | bytes 1048576 | tf_op jit(solution)/shard_map/all_to_all | solution.py:495
  72.6 326.0 %copy-start.1 = (bf16[1,8192,64]{1,2,0:T(8,128)(2,1)S(1)}, bf16[1,8192,64]{1,2,0:T(8,128)(2,1)}, u32[]{:S(2)}) copy-start(bf16[1,8192,64]{1,2,0:T(8,128)(2,1)} %param.13) | copy-start | bytes 3145732
  400.3 7.7 %copy-start.3 = (f32[1,8192]{1,0:T(1,128)S(1)}, f32[1,8192]{1,0:T(1,128)}, u32[]{:S(2)}) copy-start(f32[1,8192]{1,0:T(1,128)} %get-tuple-element.11) | copy-start | bytes 98308
  400.3 8.4 %copy-start.4 = (f32[1,512]{1,0:T(1,128)S(1)}, f32[1,512]{1,0:T(1,128)}, u32[]{:S(2)}) copy-start(f32[1,512]{1,0:T(1,128)} %get-tuple-element.13) | copy-start | bytes 6148
  400.3 9.0 %copy-start.2 = (bf16[2,16,8192]{2,1,0:T(8,128)(2,1)S(1)}, bf16[2,16,8192]{2,1,0:T(8,128)(2,1)}, u32[]{:S(2)}) copy-start(bf16[2,16,8192]{2,1,0:T(8,128)(2,1)} %get-tuple-element.10) | copy-start | bytes 1572868
Sparse Core Ops, SparseCore 0:
  20.3 32.2 all-reduce.1
